TPU v7x, 32 devices: a whole 2x2x4 slice. The times are simulated.
32 devices in a mesh: lat: 8 (over z, y), lon: 4 (over x, core).
Axes of the slice: x: 2, y: 2, z: 4, core: 2. Of those that a mesh axis runs over, the one named last changes fastest.
Arguments:
- raw_fields: bfloat16 [32, 160, 1440], P(('lat', 'lon')), may hold values from -6 to 6
- embed_weight: bfloat16 [32, 4, 4, 1024], replicated, may hold values from -0.25 to 0.25
- embed_bias: float32 [1024], replicated, may hold values from -3 to 3
- conv_weight: bfloat16 [3, 3, 1024, 1024], replicated, may hold values from -0.0625 to 0.0625
- conv_bias: float32 [1024], replicated, may hold values from -3 to 3
Outputs:
- features: bfloat16 [40, 360, 1024], P('lat', 'lon')
All inputs are finite; a program needn't handle non-finite values.
Results may differ from a plain program's by a relative error of at most 0.0049.
Values may be sent and summed in bfloat16 or wider, within the bound.
A program may use at most 192 MiB of HBM per device.

v0:
```python
import jax
import jax.numpy as jnp
from jax import lax
from jax.sharding import PartitionSpec as P

PATCH = 4


def with_halo(value, sides, width, wrap):
    for axis, dim in sides:
        count, length = (lax.axis_size(axis), value.shape[dim])
        up = [(i, (i + 1) % count) for i in range(count if wrap else count - 1)]
        down = [(j, i) for i, j in up]
        last = lax.slice_in_dim(value, length - width, length, axis=dim)
        leading = lax.slice_in_dim(value, 0, width, axis=dim)
        before = lax.ppermute(last, axis, up)
        after = lax.ppermute(leading, axis, down)
        value = jnp.concatenate([before, value, after], axis=dim)
    return value


def per_device(raw_fields, embed_weight, embed_bias, conv_weight, conv_bias):
    lat_count = lax.axis_size("lat")
    lon_count = lax.axis_size("lon")
    var_dev, height, breadth = raw_fields.shape
    tile_height = height // lat_count
    tile_breadth = breadth // lon_count
    pieces = raw_fields.reshape(var_dev, lat_count, tile_height, lon_count, tile_breadth)
    pieces = pieces.transpose(1, 3, 0, 2, 4).reshape(
        lat_count * lon_count * var_dev, tile_height, tile_breadth
    )
    tile_block = lax.all_to_all(pieces, ("lat", "lon"), split_axis=0, concat_axis=0, tiled=True)
    patch_rows = tile_height // PATCH
    patch_cols = tile_breadth // PATCH
    grid_blocks = tile_block.reshape(-1, patch_rows, PATCH, patch_cols, PATCH)
    embedded = jnp.einsum(
        "vaibj,vijd->abd", grid_blocks, embed_weight, preferred_element_type=jnp.float32
    )
    embedded = (embedded + embed_bias).astype(jnp.bfloat16)
    channels = embedded.shape[2]
    lon_padded = with_halo(embedded, (("lon", 1),), 1, True)
    padded = with_halo(lon_padded, (("lat", 0),), 1, False)
    summed = jnp.zeros((patch_rows * patch_cols, channels), jnp.float32)
    for step_row in range(3):
        for step_col in range(3):
            window = padded[
                step_row : step_row + patch_rows, step_col : step_col + patch_cols
            ].reshape(-1, channels)
            summed = summed + jnp.dot(
                window, conv_weight[step_row, step_col], preferred_element_type=jnp.float32
            )
    summed = summed + conv_bias
    result = jax.nn.gelu(summed, approximate=False).astype(jnp.bfloat16)
    return result.reshape(patch_rows, patch_cols, channels)


def solution(mesh):
    return jax.shard_map(
        per_device,
        mesh=mesh,
        in_specs=(P(("lat", "lon"), None, None), P(), P(), P(), P()),
        out_specs=P("lat", "lon", None),
        check_vma=False,
    )
```

profile of v0, /device:TPU:0, one launch (start us, length us, event | category | flops | bytes accessed | tf_op | source)
XLA Modules:
  0.0 93.1 jit_solution(10198314950242931978)
XLA Ops:
  0.0 1.5 %reshape.41 = bf16[1,8,20,4,360]{4,3,2,1,0:T(4,128)(2,1)S(1)} reshape(bf16[1,160,1440]{2,1,0:T(8,128)(2,1)} %param.5) | data formatting | bytes 921600 | tf_op jit(solution)/shard_map/reshape | solution.py:28
  1.5 0.2 copy.27
  1.9 23.9 %all_to_all.5 = bf16[32,20,360]{2,1,0:T(8,128)(2,1)S(1)} all-to-all(bf16[32,20,360]{2,1,0:T(8,128)(2,1)S(1)} %bitcast.52), channel_id=1, replica_groups=mesh['lat'=8,'lon'=4] {'lat','lon'}, dimensions={0} | all-to-all | bytes 921600 | tf_op jit(solution)/shard_map/all_to_all | solution.py:32
  25.8 1.3 %copy.13 = bf16[32,20,360]{0,2,1:T(8,128)(2,1)S(1)} copy(bf16[32,20,360]{2,1,0:T(8,128)(2,1)S(1)} %all_to_all.5) | data formatting | bytes 921600 | tf_op jit(solution)/shard_map/all_to_all | solution.py:32
  27.2 2.8 %fusion.27 = bf16[5,90,1024]{2,1,0:T(8,128)(2,1)S(1)} fusion(bf16[32,5,4,90,4]{0,4,3,2,1:T(4,128)(2,1)S(1)} %bitcast.54, bf16[32,4,4,1024]{3,2,1,0:T(4,128)(2,1)} %param.6, f32[1024]{0:T(1024)S(1)} %copy-done.5), kind=kOutput, calls=%fused_computation.29 | convolution fusion | flops 472780800 | bytes 2435072 | tf_op jit(solution)/shard_map/vaibj,vijd->abd/dot_general | solution.py:36
  30.1 0.2 reshape.48
  30.3 1.7 %collective-permute-start.1 = (bf16[5,1,1024]{2,1,0:T(2,128)(2,1)S(1)}, bf16[5,1,1024]{2,1,0:T(2,128)(2,1)S(1)}, u32[]{:S(2)}, u32[]{:S(2)}) collective-permute-start(bf16[5,1,1024]{2,1,0:T(2,128)(2,1)S(1)} %get-tuple-element.18), channel_id=1, source_target_pairs={{1,0},{2,1},{3,2},{0,3},{5,4},{6,5},{7,6},{4,7},{9,8},{10,9},{11,1... | collective-permute-start | bytes 30728 | tf_op jit(solution)/shard_map/ppermute | solution.py:17
  32.1 4.0 %fusion.8 = f32[450,1024]{1,0:T(8,128)} fusion(bf16[450,1024]{1,0:T(8,128)(2,1)S(1)} %reshape.48, bf16[3,3,1024,1024]{3,2,1,0:T(8,128)(2,1)} %param.8), kind=kOutput, calls=%fused_computation.9 | convolution fusion | flops 943718400 | bytes 4861952 | tf_op jit(solution)/shard_map/dot_general | solution.py:49
  36.1 0.8 pad_maximum_fusion.5
  36.9 3.2 %collective-permute-start.2 = (bf16[1,92,1024]{2,1,0:T(8,128)(2,1)}, bf16[1,92,1024]{2,1,0:T(8,128)(2,1)S(1)}, u32[]{:S(2)}, u32[]{:S(2)}) collective-permute-start(bf16[1,92,1024]{2,1,0:T(8,128)(2,1)} %get-tuple-element.13), channel_id=1, source_target_pairs={{0,4},{4,8},{8,12},{12,16},{16,20},{20,24},{24,28},{1,5},{5,9},{9,... | collective-permute-start | bytes 565256 | tf_op jit(solution)/shard_map/ppermute | solution.py:16
  40.1 1.3 %collective-permute-start.3 = (bf16[1,92,1024]{2,1,0:T(8,128)(2,1)S(1)}, bf16[1,92,1024]{2,1,0:T(8,128)(2,1)S(1)}, u32[]{:S(2)}, u32[]{:S(2)}) collective-permute-start(bf16[1,92,1024]{2,1,0:T(8,128)(2,1)S(1)} %get-tuple-element.14), channel_id=1, source_target_pairs={{4,0},{8,4},{12,8},{16,12},{20,16},{24,20},{28,24},{5,1},{9,5},{13... | collective-permute-start | bytes 565256 | tf_op jit(solution)/shard_map/ppermute | solution.py:17
  41.4 0.5 pad_maximum_fusion.2
  41.9 1.1 %reshape.47 = bf16[450,1024]{1,0:T(8,128)(2,1)} reshape(bf16[5,90,1024]{2,1,0:T(8,128)(2,1)S(1)} %get-tuple-element.15) | data formatting | bytes 1843200 | tf_op jit(solution)/shard_map/reshape | solution.py:48
  43.0 4.3 %fusion.10 = f32[450,1024]{1,0:T(8,128)} fusion(bf16[450,1024]{1,0:T(8,128)(2,1)} %reshape.47, bf16[3,3,1024,1024]{3,2,1,0:T(8,128)(2,1)} %param.8), kind=kOutput, calls=%fused_computation.11 | convolution fusion | flops 943718400 | bytes 4874240 | tf_op jit(solution)/shard_map/dot_general | solution.py:49
  47.3 0.2 reshape.49
  47.6 4.0 %fusion.6 = f32[450,1024]{1,0:T(8,128)} fusion(bf16[450,1024]{1,0:T(8,128)(2,1)S(1)} %reshape.49, bf16[3,3,1024,1024]{3,2,1,0:T(8,128)(2,1)} %param.8), kind=kOutput, calls=%fused_computation.7 | convolution fusion | flops 943718400 | bytes 4861952 | tf_op jit(solution)/shard_map/dot_general | solution.py:49
  51.5 0.5 maximum_maximum_fusion
  52.0 2.5 %fusion.46 = (bf16[5,90,1024]{2,1,0:T(8,128)(2,1)}, bf16[5,90,1024]{2,1,0:T(8,128)(2,1)}, bf16[5,90,1024]{2,1,0:T(8,128)(2,1)}, bf16[5,90,1024]{2,1,0:T(8,128)(2...) fusion(bf16[6,92,1024]{2,1,0:T(8,128)(2,1)S(1)} %get-tuple-element.12, ...), kind=kLoop, calls=%fused_computation.61 | loop fusion | bytes 11059200 | tf_op jit(solution)/shard_map/slice | solution.py:46
  54.6 2.3 %reshape.52 = bf16[450,1024]{1,0:T(8,128)(2,1)} reshape(bf16[5,90,1024]{2,1,0:T(8,128)(2,1)} %get-tuple-element.5) | data formatting | bytes 1843200 | tf_op jit(solution)/shard_map/reshape | solution.py:48
  56.8 2.3 %reshape.51 = bf16[450,1024]{1,0:T(8,128)(2,1)} reshape(bf16[5,90,1024]{2,1,0:T(8,128)(2,1)} %get-tuple-element.6) | data formatting | bytes 1843200 | tf_op jit(solution)/shard_map/reshape | solution.py:48
  59.1 4.3 %fusion.2 = f32[450,1024]{1,0:T(8,128)} fusion(bf16[450,1024]{1,0:T(8,128)(2,1)} %reshape.51, bf16[3,3,1024,1024]{3,2,1,0:T(8,128)(2,1)} %param.8), kind=kOutput, calls=%fused_computation.3 | convolution fusion | flops 943718400 | bytes 4874240 | tf_op jit(solution)/shard_map/dot_general | solution.py:49
  63.4 2.3 %reshape.50 = bf16[450,1024]{1,0:T(8,128)(2,1)} reshape(bf16[5,90,1024]{2,1,0:T(8,128)(2,1)} %get-tuple-element.7) | data formatting | bytes 1843200 | tf_op jit(solution)/shard_map/reshape | solution.py:48
  65.6 4.3 %fusion.4 = f32[450,1024]{1,0:T(8,128)} fusion(bf16[450,1024]{1,0:T(8,128)(2,1)} %reshape.50, bf16[3,3,1024,1024]{3,2,1,0:T(8,128)(2,1)} %param.8), kind=kOutput, calls=%fused_computation.5 | convolution fusion | flops 943718400 | bytes 4874240 | tf_op jit(solution)/shard_map/dot_general | solution.py:49
  70.0 1.1 %reshape.44 = bf16[450,1024]{1,0:T(8,128)(2,1)} reshape(bf16[5,90,1024]{2,1,0:T(8,128)(2,1)S(1)} %get-tuple-element.19) | data formatting | bytes 1843200 | tf_op jit(solution)/shard_map/reshape | solution.py:48
  71.1 4.4 %fusion.16 = f32[450,1024]{1,0:T(8,128)} fusion(bf16[450,1024]{1,0:T(8,128)(2,1)} %reshape.44, bf16[3,3,1024,1024]{3,2,1,0:T(8,128)(2,1)} %param.8), kind=kOutput, calls=%fused_computation.17 | convolution fusion | flops 943718400 | bytes 4874240 | tf_op jit(solution)/shard_map/dot_general | solution.py:49
  75.5 0.2 reshape.46
  75.7 4.0 %fusion.12 = f32[450,1024]{1,0:T(8,128)} fusion(bf16[450,1024]{1,0:T(8,128)(2,1)S(1)} %reshape.46, bf16[3,3,1024,1024]{3,2,1,0:T(8,128)(2,1)} %param.8), kind=kOutput, calls=%fused_computation.13 | convolution fusion | flops 943718400 | bytes 4861952 | tf_op jit(solution)/shard_map/dot_general | solution.py:49
  79.7 0.2 reshape.45
  79.9 2.9 %fusion.14 = f32[450,1024]{1,0:T(8,128)S(1)} fusion(bf16[450,1024]{1,0:T(8,128)(2,1)S(1)} %reshape.45, bf16[3,3,1024,1024]{3,2,1,0:T(8,128)(2,1)} %param.8), kind=kOutput, calls=%fused_computation.15 | convolution fusion | flops 943718400 | bytes 4861952 | tf_op jit(solution)/shard_map/dot_general | solution.py:49
  82.9 0.6 copy-done.9
  83.5 8.5 %fusion.32 = bf16[450,1024]{1,0:T(8,128)(2,1)S(1)} fusion(f32[450,1024]{1,0:T(8,128)} %fusion.2, f32[450,1024]{1,0:T(8,128)} %fusion.4, f32[450,1024]{1,0:T(8,128)S(1)} %copy-done.9, f32[450,1024]{1,0:T(8,128)S(1)} %copy-done.7, f32[450,1024]{1,0:T(8,128)S(1)} %copy-done.8, f32[450,1024]{1,0:T(8,128)} %fusion.12, f32[450,1024]{1,0:T(8,128)} %fusion.16, ...), kind=kOutput, calls=%fused_computation.34 | convolution fusion | flops 977817600 | bytes 18788352 | tf_op jit(solution)/shard_map/dot_general | solution.py:49
  91.9 1.2 %reshape.53 = bf16[5,90,1024]{2,1,0:T(8,128)(2,1)} reshape(bf16[450,1024]{1,0:T(8,128)(2,1)S(1)} %fusion.32) | data formatting | bytes 1843200 | tf_op jit(solution)/shard_map/reshape | solution.py:54
  (26 shorter events, 0.4 us)
Async XLA Ops:
  1.9 25.3 %copy-start.5 = (f32[1024]{0:T(1024)S(1)}, f32[1024]{0:T(1024)}, u32[]{:S(2)}) copy-start(f32[1024]{0:T(1024)} %param.7) | copy-start | bytes 12292
  30.3 5.8 %collective-permute-start = (bf16[5,1,1024]{2,1,0:T(2,128)(2,1)S(1)}, bf16[5,1,1024]{2,1,0:T(2,128)(2,1)S(1)}, u32[]{:S(2)}, u32[]{:S(2)}) collective-permute-start(bf16[5,1,1024]{2,1,0:T(2,128)(2,1)S(1)} %get-tuple-element.17), channel_id=1, source_target_pairs={{0,1},{1,2},{2,3},{3,0},{4,5},{5,6},{6,7},{7,4},{8,9},{9,10},{10,1... | collective-permute-start | bytes 30728 | tf_op jit(solution)/shard_map/ppermute | solution.py:16
  30.3 5.7 %collective-permute-start.1 = (bf16[5,1,1024]{2,1,0:T(2,128)(2,1)S(1)}, bf16[5,1,1024]{2,1,0:T(2,128)(2,1)S(1)}, u32[]{:S(2)}, u32[]{:S(2)}) collective-permute-start(bf16[5,1,1024]{2,1,0:T(2,128)(2,1)S(1)} %get-tuple-element.18), channel_id=1, source_target_pairs={{1,0},{2,1},{3,2},{0,3},{5,4},{6,5},{7,6},{4,7},{9,8},{10,9},{11,1... | collective-permute-start | bytes 30728 | tf_op jit(solution)/shard_map/ppermute | solution.py:17
  36.1 5.8 %copy-start.1 = (bf16[5,1,1024]{2,1,0:T(2,128)(2,1)}, bf16[5,1,1024]{2,1,0:T(2,128)(2,1)S(1)}, u32[]{:S(2)}) copy-start(bf16[5,1,1024]{2,1,0:T(2,128)(2,1)S(1)} %collective-permute-done) | copy-start | bytes 30724
  36.1 5.8 %copy-start.3 = (bf16[5,1,1024]{2,1,0:T(2,128)(2,1)}, bf16[5,1,1024]{2,1,0:T(2,128)(2,1)S(1)}, u32[]{:S(2)}) copy-start(bf16[5,1,1024]{2,1,0:T(2,128)(2,1)S(1)} %collective-permute-done.1) | copy-start | bytes 30724
  36.9 14.6 %collective-permute-start.2 = (bf16[1,92,1024]{2,1,0:T(8,128)(2,1)}, bf16[1,92,1024]{2,1,0:T(8,128)(2,1)S(1)}, u32[]{:S(2)}, u32[]{:S(2)}) collective-permute-start(bf16[1,92,1024]{2,1,0:T(8,128)(2,1)} %get-tuple-element.13), channel_id=1, source_target_pairs={{0,4},{4,8},{8,12},{12,16},{16,20},{20,24},{24,28},{1,5},{5,9},{9,... | collective-permute-start | bytes 565256 | tf_op jit(solution)/shard_map/ppermute | solution.py:16
  40.1 11.4 %collective-permute-start.3 = (bf16[1,92,1024]{2,1,0:T(8,128)(2,1)S(1)}, bf16[1,92,1024]{2,1,0:T(8,128)(2,1)S(1)}, u32[]{:S(2)}, u32[]{:S(2)}) collective-permute-start(bf16[1,92,1024]{2,1,0:T(8,128)(2,1)S(1)} %get-tuple-element.14), channel_id=1, source_target_pairs={{4,0},{8,4},{12,8},{16,12},{20,16},{24,20},{28,24},{5,1},{9,5},{13... | collective-permute-start | bytes 565256 | tf_op jit(solution)/shard_map/ppermute | solution.py:17
  47.5 4.0 %copy-start.2 = (bf16[5,1,1024]{2,1,0:T(2,128)(2,1)S(1)}, bf16[5,1,1024]{2,1,0:T(2,128)(2,1)}, u32[]{:S(2)}) copy-start(bf16[5,1,1024]{2,1,0:T(2,128)(2,1)} %copy-done.1) | copy-start | bytes 30724
  47.5 4.0 %copy-start.4 = (bf16[5,1,1024]{2,1,0:T(2,128)(2,1)S(1)}, bf16[5,1,1024]{2,1,0:T(2,128)(2,1)}, u32[]{:S(2)}) copy-start(bf16[5,1,1024]{2,1,0:T(2,128)(2,1)} %copy-done.3) | copy-start | bytes 30724
  79.9 2.9 %copy-start = (bf16[450,1024]{1,0:T(8,128)(2,1)S(1)}, bf16[450,1024]{1,0:T(8,128)(2,1)}, u32[]{:S(2)}) copy-start(bf16[450,1024]{1,0:T(8,128)(2,1)} %reshape.52) | copy-start | bytes 2764804
  79.9 2.9 %copy-start.6 = (f32[1024]{0:T(1024)S(1)}, f32[1024]{0:T(1024)}, u32[]{:S(2)}) copy-start(f32[1024]{0:T(1024)} %param.9) | copy-start | bytes 12292
  79.9 2.9 %copy-start.7 = (f32[450,1024]{1,0:T(8,128)S(1)}, f32[450,1024]{1,0:T(8,128)}, u32[]{:S(2)}) copy-start(f32[450,1024]{1,0:T(8,128)} %fusion.8) | copy-start | bytes 5529604
  79.9 3.0 %copy-start.8 = (f32[450,1024]{1,0:T(8,128)S(1)}, f32[450,1024]{1,0:T(8,128)}, u32[]{:S(2)}) copy-start(f32[450,1024]{1,0:T(8,128)} %fusion.10) | copy-start | bytes 5529604
  79.9 3.5 %copy-start.9 = (f32[450,1024]{1,0:T(8,128)S(1)}, f32[450,1024]{1,0:T(8,128)}, u32[]{:S(2)}) copy-start(f32[450,1024]{1,0:T(8,128)} %fusion.6) | copy-start | bytes 5529604
where the time goes:
time: 94.2 us; the launch traced here: 93.1 us
  matrix products  43.4 us (46%)
  blocking collectives  23.9 us (25%)
  local copies, waits for them, and re-layouts  17.5 us (19%)
  starting transfers between devices  6.3 us (7%)
  other arithmetic  1.77 us (2%)
    dot_general x9, matrix products, per_device(): jnp.dot(window, conv_weight[step_row, step_col], preferred_element_type=j...  40.5 us
    all_to_all x1, blocking collectives, per_device(): lax.all_to_all(pieces, ('lat', 'lon'), split_axis=0, concat_axis=0, tiled...  23.9 us
    reshape x9, local copies, waits for them, and re-layouts, per_device(): window = padded[step_row:step_row + patch_rows, step_col:step_col + patch...  9.87 us
    ppermute x2, starting transfers between devices, with_halo(): before = lax.ppermute(last, axis, up)  3.27 us
    ppermute x2, starting transfers between devices, with_halo(): after = lax.ppermute(leading, axis, down)  3.02 us
    dot_general x1, matrix products, per_device(): jnp.einsum('vaibj,vijd->abd', grid_blocks, embed_weight, preferred_elemen...  2.83 us
    slice x1, local copies, waits for them, and re-layouts, per_device(): padded[step_row:step_row + patch_rows, step_col:step_col + patch_cols]  2.52 us
  transfers between devices with their start and end apart: 4, of which 0 were waited for; matrix products, arithmetic and copies ran while one was open for 15% of the time, Pallas kernels for 0%

commit v1 on v0

v1 whole, which is shorter than its diff:
```python
import functools

import jax
import jax.numpy as jnp
from jax import lax
from jax.experimental import pallas as pl
from jax.experimental.pallas import tpu as pltpu
from jax.sharding import PartitionSpec as P

PATCH = 4
LANES = 128
CELLS = PATCH * PATCH
MESH = pl.DeviceIdType.MESH


def kernel(
    dims,
    raw_hbm, ew_hbm, eb_ref, cw_hbm, cb_ref,
    out_ref,
    raw, field, sides, send, send_halo, recv, recv_halo, ew_raw, ew, cw, taps,
    raw_sem, ew_sem, cw_sem, send_sem, recv_sem, hsend_sem, hrecv_sem,
):
    lat_n, lon_n, height, breadth, rows, cols, width = dims
    total = lat_n * lon_n
    lat = lax.axis_index("lat")
    lon = lax.axis_index("lon")
    me = lat * lon_n + lon
    row_slots = taps.shape[0] // (rows + 2)
    spare = LANES - row_slots

    raw_copy = pltpu.make_async_copy(raw_hbm.at[0], raw, raw_sem)
    raw_copy.start()

    def peer(step):
        k = step // lon_n
        r = step % lon_n
        off = lat_n // 2 + (2 * (k % 2) - 1) * ((k + 1) // 2)
        return (lat + off + lat_n) % lat_n, (lon + r + 1) % lon_n

    barrier = pltpu.get_barrier_semaphore()

    @pl.loop(0, total - 1)
    def _(step):
        a, b = peer(step)
        pl.semaphore_signal(barrier, inc=1, device_id=(a, b), device_id_type=MESH)

    ew_copy = pltpu.make_async_copy(ew_hbm, ew_raw, ew_sem)
    ew_copy.start()
    cw_copies = []
    for p in range(3):
        for q in range(3):
            copy = pltpu.make_async_copy(cw_hbm.at[p, q], cw.at[p, q], cw_sem.at[3 * p + q])
            copy.start()
            cw_copies.append(copy)

    whole = pl.cdiv(breadth, LANES)
    patches = breadth // PATCH
    raw_copy.wait()
    main_lanes = (breadth // LANES) * LANES
    field[:, :main_lanes] = raw[:, :main_lanes]
    if main_lanes < breadth:
        tail = raw[:, main_lanes:]
        fill = jnp.zeros((height, whole * LANES - breadth), jnp.bfloat16)
        field[:, main_lanes:] = jnp.concatenate([tail, fill], axis=1)

    group = min(lat_n, 8)
    group_rows = group * rows * PATCH
    block = group * CELLS
    lane = lax.broadcasted_iota(jnp.int32, (1, PATCH * LANES), 1)
    slot = lane % LANES
    cell = lane // LANES
    m = lax.broadcasted_iota(jnp.int32, (rows * block, 1), 0)
    target = (
        (m % PATCH) * group_rows
        + ((m // CELLS) % group) * (rows * PATCH)
        + (m // block) * PATCH
        + (m // PATCH) % PATCH
    )
    c = lax.broadcasted_iota(jnp.int32, (rows * block, PATCH * group_rows), 1)
    pick_rows = jnp.where(c == target, 1.0, 0.0).astype(jnp.bfloat16)
    for g in range(lat_n // group):
        band = field[g * group_rows : (g + 1) * group_rows, :]
        for l in range(lon_n):
            wanted = [
                (PATCH * ((cols * l - 1 + s) % patches)) // LANES for s in range(cols + 2)
            ]
            used = sorted(set(wanted))
            used += [
                b for b in sorted({(PATCH * ((cols * l - 1 + s) % patches) + PATCH - 1) // LANES for s in range(cols + 2)})
                if b not in used
            ]
            patch = (cols * l - 1 + slot + patches) % patches
            column = jnp.where(slot < cols + 2, PATCH * patch + cell, -1)
            picks = []
            parts = []
            for b in used:
                k = lax.broadcasted_iota(jnp.int32, (LANES, PATCH * LANES), 0) + b * LANES
                picks.append(jnp.where(k == column, 1.0, 0.0).astype(jnp.bfloat16))
                parts.append(band[:, b * LANES : (b + 1) * LANES])
            found = jnp.dot(
                jnp.concatenate(parts, axis=1),
                jnp.concatenate(picks, axis=0),
                preferred_element_type=jnp.float32,
            ).astype(jnp.bfloat16)
            for j in range(PATCH):
                sides[j * group_rows : (j + 1) * group_rows, l * LANES : (l + 1) * LANES] = (
                    found[:, j * LANES : (j + 1) * LANES]
                )
        tiles = jnp.dot(pick_rows, sides[...], preferred_element_type=jnp.float32)
        low = lax.broadcasted_iota(jnp.int32, (block, LANES), 1) < row_slots
        for l in range(lon_n):
            column = tiles[:, l * LANES : (l + 1) * LANES]
            per_row = [column[a * block : (a + 1) * block] for a in range(rows)]
            last = per_row[rows - 1]
            for a in range(rows - 1):
                moved = last if a * spare >= row_slots else pltpu.roll(
                    last, row_slots - a * spare, 1
                )
                packed = jnp.where(low, per_row[a], moved).astype(jnp.bfloat16)
                send[g * group : (g + 1) * group, l, :, a * LANES : (a + 1) * LANES] = (
                    packed.reshape(group, CELLS, LANES)
                )
            first = per_row[0].astype(jnp.bfloat16).reshape(group, CELLS, LANES)
            final = last.astype(jnp.bfloat16).reshape(group, CELLS, LANES)
            send_halo[g * group + 1 : (g + 1) * group + 1, l, :, :LANES] = final
            if g == 0:
                send_halo[0, l, :, :LANES] = jnp.zeros((CELLS, LANES), jnp.bfloat16)
                send_halo[: group - 1, l, :, LANES:] = first[1:]
            else:
                send_halo[g * group - 1 : (g + 1) * group - 1, l, :, LANES:] = first
            if g == lat_n // group - 1:
                send_halo[lat_n - 1, l, :, LANES:] = jnp.zeros((CELLS, LANES), jnp.bfloat16)

    pl.semaphore_wait(barrier, total - 1)

    def exchange(source, dest, out_sem, in_sem):
        @pl.loop(0, total - 1)
        def _(step):
            a, b = peer(step)
            pltpu.make_async_remote_copy(
                src_ref=source.at[a, b],
                dst_ref=dest.at[me],
                send_sem=out_sem,
                recv_sem=in_sem,
                device_id=(a, b),
                device_id_type=MESH,
            ).start()

        pltpu.make_async_copy(source.at[lat, lon], dest.at[me], in_sem).start()

    exchange(send, recv, send_sem, recv_sem)

    ew_copy.wait()
    for i in range(PATCH):
        ew[:, PATCH * i : PATCH * (i + 1), :] = ew_raw[:, i]
    pltpu.make_async_copy(recv, recv, recv_sem).wait()
    exchange(send_halo, recv_halo, hsend_sem, hrecv_sem)

    def place(row, n, tokens):
        lanes = slice(n, n + tokens.shape[1])
        start = row * row_slots
        for q in range(3):
            shifted = tokens if q == 0 else pltpu.roll(tokens, row_slots - q, 0)
            taps[start : start + row_slots, q * width + lanes.start : q * width + lanes.stop] = (
                shifted.astype(jnp.bfloat16)
            )

    step_n = 256
    x = recv[...].reshape(total * CELLS, recv.shape[2]).T
    for n in range(0, width, step_n):
        weights = ew[:, :, n : n + step_n].reshape(total * CELLS, step_n)
        e = jnp.dot(x, weights, preferred_element_type=jnp.float32) + eb_ref[:, n : n + step_n]
        chunks = []
        for a in range(rows - 1):
            place(a + 1, n, e[a * LANES : a * LANES + row_slots])
            if a * spare < row_slots:
                chunks.append(e[a * LANES + row_slots : (a + 1) * LANES])
        place(rows, n, jnp.concatenate(chunks, axis=0)[:row_slots])

    for copy in cw_copies:
        copy.wait()

    def conv(first_rows):
        @pl.loop(0, width // step_n)
        def _(block_n):
            n = pl.multiple_of(block_n * step_n, step_n)
            summed = None
            for p in range(3):
                spans = [
                    taps[(a + p) * row_slots : (a + p + count) * row_slots, :]
                    for a, count in first_rows
                ]
                left = spans[0] if len(spans) == 1 else jnp.concatenate(spans, axis=0)
                weights = cw[p, :, :, pl.ds(n, step_n)].reshape(3 * width, step_n)
                part = jnp.dot(left, weights, preferred_element_type=jnp.float32)
                summed = part if summed is None else summed + part
            summed = summed + cb_ref[:, pl.ds(n, step_n)]
            result = 0.5 * summed * (1.0 + lax.erf(summed * (0.5 ** 0.5)))
            result = result.astype(jnp.bfloat16)
            at = 0
            for a, count in first_rows:
                for k in range(count):
                    out_ref[a + k, :, pl.ds(n, step_n)] = result[at : at + cols]
                    at += row_slots

    conv([(1, rows - 2)])

    pltpu.make_async_copy(recv_halo, recv_halo, hrecv_sem).wait()
    x = recv_halo[...].reshape(total * CELLS, recv_halo.shape[2]).T
    top = jnp.where(lat > 0, 1.0, 0.0)
    bottom = jnp.where(lat < lat_n - 1, 1.0, 0.0)
    for n in range(0, width, step_n):
        weights = ew[:, :, n : n + step_n].reshape(total * CELLS, step_n)
        e = jnp.dot(x, weights, preferred_element_type=jnp.float32) + eb_ref[:, n : n + step_n]
        place(0, n, e[:row_slots] * top)
        place(rows + 1, n, e[LANES : LANES + row_slots] * bottom)
    conv([(0, 1), (rows - 1, 1)])

    sent = pl.ds(0, total - 1)
    pltpu.make_async_copy(recv.at[sent], recv.at[sent], send_sem).wait()
    pltpu.make_async_copy(recv_halo.at[sent], recv_halo.at[sent], hsend_sem).wait()


def per_device(raw_fields, embed_weight, embed_bias, conv_weight, conv_bias):
    lat_n = lax.axis_size("lat")
    lon_n = lax.axis_size("lon")
    total = lat_n * lon_n
    var_dev, height, breadth = raw_fields.shape
    assert var_dev == 1
    rows = height // lat_n // PATCH
    cols = breadth // lon_n // PATCH
    width = embed_weight.shape[3]
    row_slots = (cols + 2 + 15) // 16 * 16
    spare = LANES - row_slots
    assert row_slots < LANES and spare * (rows - 1) >= cols + 2
    dims = (lat_n, lon_n, height, breadth, rows, cols, width)
    group = min(lat_n, 8)
    bf16 = jnp.bfloat16
    whole = pl.cdiv(breadth, LANES) * LANES
    any_space = pl.BlockSpec(memory_space=pl.ANY)
    vmem = pl.BlockSpec(memory_space=pltpu.VMEM)
    return pl.pallas_call(
        functools.partial(kernel, dims),
        out_shape=jax.ShapeDtypeStruct((rows, cols, width), bf16),
        in_specs=[any_space, any_space, vmem, any_space, vmem],
        out_specs=vmem,
        scratch_shapes=[
            pltpu.VMEM((height, breadth), bf16),
            pltpu.VMEM((height, whole), bf16),
            pltpu.VMEM((PATCH * group * rows * PATCH, lon_n * LANES), bf16),
            pltpu.VMEM((lat_n, lon_n, CELLS, (rows - 1) * LANES), bf16),
            pltpu.VMEM((lat_n + 1, lon_n, CELLS, 2 * LANES), bf16),
            pltpu.VMEM((total, CELLS, (rows - 1) * LANES), bf16),
            pltpu.VMEM((total, CELLS, 2 * LANES), bf16),
            pltpu.VMEM((total, PATCH, PATCH, width), bf16),
            pltpu.VMEM((total, CELLS, width), bf16),
            pltpu.VMEM((3, 3, width, width), bf16),
            pltpu.VMEM(((rows + 2) * row_slots, 3 * width), bf16),
            pltpu.SemaphoreType.DMA,
            pltpu.SemaphoreType.DMA,
            pltpu.SemaphoreType.DMA((9,)),
            pltpu.SemaphoreType.DMA,
            pltpu.SemaphoreType.DMA,
            pltpu.SemaphoreType.DMA,
            pltpu.SemaphoreType.DMA,
        ],
        compiler_params=pltpu.CompilerParams(
            collective_id=0, has_side_effects=True, vmem_limit_bytes=60 * 1024 * 1024
        ),
        name="tiles",
    )(
        raw_fields,
        embed_weight,
        embed_bias.reshape(1, width),
        conv_weight,
        conv_bias.reshape(1, width),
    )


def solution(mesh):
    return jax.shard_map(
        per_device,
        mesh=mesh,
        in_specs=(P(("lat", "lon"), None, None), P(), P(), P(), P()),
        out_specs=P("lat", "lon", None),
        check_vma=False,
    )
```

time: 94.2 us -> 36.8 us (0.39)
  matrix products: 43.4 us -> 0 us
  Pallas kernels: 0 us -> 34.4 us
  blocking collectives: 23.9 us -> 0 us
  local copies, waits for them, and re-layouts: 17.5 us -> 2.24 us
  starting transfers between devices: 6.3 us -> 0 us
  other arithmetic: 1.77 us -> 0 us
    dot_general x10 -> x0, matrix products: 43.4 us -> none  [the longest x9 40.5 us: per_device(): jnp.dot(window, conv_weight[step_row, step_col], preferred_element_type=j...]
    pallas_call x0 -> x1, Pallas kernels: none -> 34.4 us  [per_device(): pl.pallas_call(functools.partial(kernel, dims), out_shape=jax.ShapeDtypeS...]
    all_to_all x1 -> x0, blocking collectives: 23.9 us -> none  [per_device(): lax.all_to_all(pieces, ('lat', 'lon'), split_axis=0, concat_axis=0, tiled...]
    reshape x13 -> x0, local copies, waits for them, and re-layouts: 12.9 us -> none  [the longest x9 9.87 us: per_device(): window = padded[step_row:step_row + patch_rows, step_col:step_col + patch...]
    ppermute x4 -> x0, starting transfers between devices: 6.3 us -> none  [the longest x2 3.27 us: with_halo(): before = lax.ppermute(last, axis, up)]
    slice x2 -> x0, local copies, waits for them, and re-layouts: 2.56 us -> none  [the longest x1 2.52 us: per_device(): padded[step_row:step_row + patch_rows, step_col:step_col + patch_cols]]
    unnamed x20 -> x1, local copies, waits for them, and re-layouts: 0.67 us -> 2.24 us
    all_to_all x1 -> x0, local copies, waits for them, and re-layouts: 1.33 us -> none  [per_device(): lax.all_to_all(pieces, ('lat', 'lon'), split_axis=0, concat_axis=0, tiled...]
  transfers between devices with their start and end apart: 4 -> 0, of which waited for: 0 -> 0; matrix products, arithmetic and copies ran while one was open for 15% -> 0% of each run, Pallas kernels for 0% -> 0%
where the time goes in v1:
time: 36.8 us; the launch traced here: 36.6 us
  Pallas kernels  34.4 us (93%)
  local copies, waits for them, and re-layouts  2.24 us (6%)
    pallas_call x1, Pallas kernels, per_device(): pl.pallas_call(functools.partial(kernel, dims), out_shape=jax.ShapeDtypeS...  34.4 us
    unnamed x1, local copies, waits for them, and re-layouts  2.24 us

profile of v1, /device:TPU:0, one launch (start us, length us, event | category | flops | bytes accessed | tf_op | source)
XLA Modules:
  0.0 36.6 jit_solution(13374225808873206213)
XLA Ops:
  0.0 34.4 %tiles.1 = bf16[5,90,1024]{2,1,0:T(8,128)(2,1)} custom-call(bf16[1,160,1440]{2,1,0:T(8,128)(2,1)} %raw_hbm.1, bf16[32,4,4,1024]{3,2,1,0:T(4,128)(2,1)} %ew_hbm.1, f32[1,1024]{1,0:T(1,128)} %bitcast.2, bf16[3,3,1024,1024]{3,2,1,0:T(8,128)(2,1)} %cw_hbm.1, f32[1,1024]{1,0:T(1,128)} %bitcast.3), custom_call_target="tpu_custom_call" | custom-call | tf_op jit(solution)/shard_map/tiles/pallas_call | solution.py:242
  34.4 2.2 %copy.7 = bf16[5,90,1024]{2,1,0:T(8,128)(2,1)} copy(bf16[5,90,1024]{2,1,0:T(8,128)(2,1)} %tiles.1) | data formatting | bytes 1843200

commit v2 on v1

v2 whole, which is shorter than its diff:
```python
import functools

import jax
import jax.numpy as jnp
from jax import lax
from jax.experimental import pallas as pl
from jax.experimental.pallas import tpu as pltpu
from jax.sharding import PartitionSpec as P

PATCH = 4
LANES = 128
CELLS = PATCH * PATCH
MESH = pl.DeviceIdType.MESH


def kernel(
    dims,
    raw_hbm, ew_hbm, eb_hbm, cw_hbm, cb_hbm,
    out_ref,
    eb_ref, cb_ref, raw, sides, send, send_far, recv, recv_far, near, ew_raw, ew, cw, comb, bias, taps,
    eb_sem, cb_sem, raw_sem, ew_sem, cw_sem, send_sem, recv_sem, fsend_sem, frecv_sem, nsend_sem, nrecv_sem,
):
    lat_n, lon_n, height, breadth, rows, cols, width = dims
    total = lat_n * lon_n
    lat = lax.axis_index("lat")
    lon = lax.axis_index("lon")
    me = lat * lon_n + lon
    row_slots = taps.shape[0] // (rows + 2)
    composed = total * CELLS <= width
    tap_width = total * CELLS if composed else width
    spare = LANES - row_slots

    raw_copy = pltpu.make_async_copy(raw_hbm.at[0], raw, raw_sem)
    raw_copy.start()

    def peer(step):
        k = step // lon_n
        r = step % lon_n
        off = lat_n // 2 + (2 * (k % 2) - 1) * ((k + 1) // 2)
        return (lat + off + lat_n) % lat_n, (lon + r + 1) % lon_n

    barrier = pltpu.get_barrier_semaphore()

    @pl.loop(0, total - 1)
    def _(step):
        a, b = peer(step)
        pl.semaphore_signal(barrier, inc=1, device_id=(a, b), device_id_type=MESH)

    ew_copy = pltpu.make_async_copy(ew_hbm, ew_raw, ew_sem)
    ew_copy.start()
    bias_copies = [
        pltpu.make_async_copy(eb_hbm, eb_ref, eb_sem),
        pltpu.make_async_copy(cb_hbm, cb_ref, cb_sem),
    ]
    for copy in bias_copies:
        copy.start()
    cw_copies = []
    for p in range(3):
        for q in range(3):
            copy = pltpu.make_async_copy(cw_hbm.at[p, q], cw.at[p, q], cw_sem.at[3 * p + q])
            copy.start()
            cw_copies.append(copy)

    patches = breadth // PATCH
    group = min(lat_n, 8)
    group_rows = group * rows * PATCH
    block = group * CELLS
    lane = lax.broadcasted_iota(jnp.int32, (1, PATCH * LANES), 1)
    slot = lane % LANES
    cell = lane // LANES
    m = lax.broadcasted_iota(jnp.int32, (rows * block, 1), 0)
    target = (
        (m % PATCH) * group_rows
        + ((m // CELLS) % group) * (rows * PATCH)
        + (m // block) * PATCH
        + (m // PATCH) % PATCH
    )
    c = lax.broadcasted_iota(jnp.int32, (rows * block, PATCH * group_rows), 1)
    pick_rows = jnp.where(c == target, 1.0, 0.0).astype(jnp.bfloat16)
    pickers = []
    for l in range(lon_n):
        wanted = [PATCH * ((cols * l - 1 + s) % patches) for s in range(cols + 2)]
        used = sorted({x // LANES for w in wanted for x in (w, w + PATCH - 1)})
        patch = (cols * l - 1 + slot + patches) % patches
        column = jnp.where(slot < cols + 2, PATCH * patch + cell, -1)
        picks = []
        for b in used:
            k = lax.broadcasted_iota(jnp.int32, (LANES, PATCH * LANES), 0) + b * LANES
            picks.append(jnp.where(k == column, 1.0, 0.0).astype(jnp.bfloat16))
        pickers.append((used, jnp.concatenate(picks, axis=0)))
    raw_copy.wait()
    for g in range(lat_n // group):
        for l in range(lon_n):
            used, picks = pickers[l]
            parts = []
            for b in used:
                part = raw[
                    g * group_rows : (g + 1) * group_rows,
                    b * LANES : min((b + 1) * LANES, breadth),
                ]
                short = LANES - part.shape[1]
                if short:
                    fill = jnp.zeros((group_rows, short), jnp.bfloat16)
                    part = jnp.concatenate([part, fill], axis=1)
                parts.append(part)
            found = jnp.dot(
                jnp.concatenate(parts, axis=1), picks, preferred_element_type=jnp.float32
            ).astype(jnp.bfloat16)
            for j in range(PATCH):
                sides[j * group_rows : (j + 1) * group_rows, l * LANES : (l + 1) * LANES] = (
                    found[:, j * LANES : (j + 1) * LANES]
                )
        tiles = jnp.dot(pick_rows, sides[...], preferred_element_type=jnp.float32)
        low = lax.broadcasted_iota(jnp.int32, (block, LANES), 1) < row_slots
        for l in range(lon_n):
            column = tiles[:, l * LANES : (l + 1) * LANES]
            per_row = [column[a * block : (a + 1) * block] for a in range(rows)]
            spread = per_row[rows - 2]
            for k in range(rows - 1):
                moved = spread if k * spare >= row_slots else pltpu.roll(
                    spread, row_slots - k * spare, 1
                )
                kept = per_row[k if k < rows - 2 else rows - 1]
                packed = jnp.where(low, kept, moved).astype(jnp.bfloat16)
                send[g * group : (g + 1) * group, l, :, k * LANES : (k + 1) * LANES] = (
                    packed.reshape(group, CELLS, LANES)
                )
            first = per_row[0].astype(jnp.bfloat16).reshape(group, CELLS, LANES)
            final = per_row[rows - 1].astype(jnp.bfloat16).reshape(group, CELLS, LANES)
            for t in range(group):
                to = g * group + (t + 1 if t % 2 else t - 1)
                if 0 <= to < lat_n:
                    send_far[to, l] = final[t] if t % 2 else first[t]
            for t in (0, lat_n - 1):
                if t // group == g:
                    send_far[t, l] = jnp.zeros((CELLS, LANES), jnp.bfloat16)

    early = 0
    ew_copy.wait()
    for copy in bias_copies:
        copy.wait()
    for i in range(PATCH):
        ew[:total, PATCH * i : PATCH * (i + 1), :] = ew_raw[:, i]
    if composed:
        high = eb_ref[...].astype(jnp.bfloat16)
        rest = eb_ref[...] - high.astype(jnp.float32)
        index = lax.broadcasted_iota(jnp.int32, (CELLS, width), 0)
        both = jnp.where(index == 0, high.astype(jnp.float32), jnp.where(index == 1, rest, 0.0))
        ew[total] = both.astype(jnp.bfloat16)

        def compose(start, stop):
            @pl.loop(start, stop)
            def _(tap):
                p, q = tap // 3, tap % 3
                pltpu.make_async_copy(cw_hbm.at[p, q], cw.at[p, q], cw_sem.at[tap]).wait()
                left = ew[...].reshape((total + 1) * CELLS, width)
                for n in range(0, width, 256):
                    product = jnp.dot(
                        left, cw[p, q, :, n : n + 256], preferred_element_type=jnp.float32
                    )
                    comb[p, q, :, n : n + 256] = product[:tap_width].astype(jnp.bfloat16)
                    bias[tap, :, n : n + 256] = product[tap_width : tap_width + 8]

        compose(0, early)

    pl.semaphore_wait(barrier, total - 1)

    def exchange(source, dest, out_sem, in_sem):
        @pl.loop(0, total - 1)
        def _(step):
            a, b = peer(step)
            pltpu.make_async_remote_copy(
                src_ref=source.at[a, b],
                dst_ref=dest.at[me],
                send_sem=out_sem,
                recv_sem=in_sem,
                device_id=(a, b),
                device_id_type=MESH,
            ).start()

        pltpu.make_async_copy(source.at[lat, lon], dest.at[me], in_sem).start()

    exchange(send, recv, send_sem, recv_sem)

    if composed:
        compose(early, 9)

    pltpu.make_async_copy(recv, recv, recv_sem).wait()
    odd = lat % 2
    edge_tile = pl.multiple_of((rows - 2) * LANES * (1 - odd), LANES)
    pair_copy = pltpu.make_async_remote_copy(
        src_ref=recv.at[:, :, pl.ds(edge_tile, LANES)],
        dst_ref=near,
        send_sem=nsend_sem,
        recv_sem=nrecv_sem,
        device_id=(lat + 1 - 2 * odd, lon),
        device_id_type=MESH,
    )
    pair_copy.start()
    exchange(send_far, recv_far, fsend_sem, frecv_sem)

    def place(row, n, tokens):
        lanes = slice(n, n + tokens.shape[1])
        start = row * row_slots
        if not isinstance(start, int):
            start = pl.multiple_of(start, 16)
        for q in range(3):
            shifted = tokens if q == 0 else pltpu.roll(tokens, row_slots - q, 0)
            taps[pl.ds(start, row_slots), q * tap_width + lanes.start : q * tap_width + lanes.stop] = (
                shifted.astype(jnp.bfloat16)
            )

    step_n = 256
    kernel_weights = comb if composed else cw

    def embed(x, n):
        weights = ew[:total, :, n : n + step_n].reshape(total * CELLS, step_n)
        return jnp.dot(x, weights, preferred_element_type=jnp.float32) + eb_ref[:, n : n + step_n]

    x = recv[...].reshape(total * CELLS, recv.shape[2]).T
    for n in range(0, tap_width, step_n):
        e = x[:, n : n + step_n].astype(jnp.float32) if composed else embed(x, n)
        chunks = []
        for k in range(rows - 1):
            row = k if k < rows - 2 else rows - 1
            place(row + 1, n, e[k * LANES : k * LANES + row_slots])
            if k * spare < row_slots:
                chunks.append(e[k * LANES + row_slots : (k + 1) * LANES])
        place(rows - 1, n, jnp.concatenate(chunks, axis=0)[:row_slots])

    top = jnp.where(lat > 0, 1.0, 0.0)
    bottom = jnp.where(lat < lat_n - 1, 1.0, 0.0)
    if not composed:
        for copy in cw_copies:
            copy.wait()

    def row_bias(a, n):
        total_bias = cb_ref[:, pl.ds(n, step_n)]
        if composed:
            for p in range(3):
                part = 0.0
                for q in range(3):
                    part += bias[3 * p + q, 0:1, pl.ds(n, step_n)] + bias[3 * p + q, 1:2, pl.ds(n, step_n)]
                if a + p == 0:
                    part *= top
                if a + p == rows + 1:
                    part *= bottom
                total_bias = total_bias + part
        return total_bias

    def conv(first_rows):
        @pl.loop(0, width // (2 * step_n))
        def _(block_n):
            for half in range(2):
                n = pl.multiple_of(block_n * (2 * step_n) + half * step_n, step_n)
                summed = None
                for p in range(3):
                    spans = [
                        taps[(a + p) * row_slots : (a + p + count) * row_slots, :]
                        for a, count in first_rows
                    ]
                    left = spans[0] if len(spans) == 1 else jnp.concatenate(spans, axis=0)
                    weights = kernel_weights[p, :, :, pl.ds(n, step_n)]
                    weights = weights.reshape(3 * tap_width, step_n)
                    part = jnp.dot(left, weights, preferred_element_type=jnp.float32)
                    summed = part if summed is None else summed + part
                at = 0
                for a, count in first_rows:
                    shift = row_bias(a, n)
                    for k in range(count):
                        value = summed[at : at + row_slots] + shift
                        value = 0.5 * value * (1.0 + lax.erf(value * (0.5 ** 0.5)))
                        out_ref[a + k, :, pl.ds(n, step_n)] = value[:cols].astype(jnp.bfloat16)
                        at += row_slots

    conv([(1, rows - 2)])

    pair_copy.wait_recv()
    pltpu.make_async_copy(recv_far, recv_far, frecv_sem).wait()
    inside = top * bottom
    for source, row, scale in (
        (near, (rows + 1) * (1 - odd), None),
        (recv_far, (rows + 1) * odd, inside),
    ):
        x = source[...].reshape(total * CELLS, LANES).T[:row_slots]
        for n in range(0, tap_width, step_n):
            if composed:
                e = x[:, n : n + step_n].astype(jnp.float32)
            else:
                e = embed(x, n)
                e = e if scale is None else e * scale
            place(row, n, e)
    conv([(0, 1), (rows - 1, 1)])

    sent = pl.ds(0, total - 1)
    pltpu.make_async_copy(recv.at[sent], recv.at[sent], send_sem).wait()
    pltpu.make_async_copy(recv_far.at[sent], recv_far.at[sent], fsend_sem).wait()
    pair_copy.wait_send()


def per_device(raw_fields, embed_weight, embed_bias, conv_weight, conv_bias):
    lat_n = lax.axis_size("lat")
    lon_n = lax.axis_size("lon")
    total = lat_n * lon_n
    var_dev, height, breadth = raw_fields.shape
    assert var_dev == 1 and lat_n % 2 == 0
    rows = height // lat_n // PATCH
    cols = breadth // lon_n // PATCH
    width = embed_weight.shape[3]
    row_slots = (cols + 2 + 15) // 16 * 16
    spare = LANES - row_slots
    assert row_slots < LANES and spare * (rows - 1) >= cols + 2
    dims = (lat_n, lon_n, height, breadth, rows, cols, width)
    group = min(lat_n, 8)
    bf16 = jnp.bfloat16
    composed = total * CELLS <= width
    tap_width = total * CELLS if composed else width
    any_space = pl.BlockSpec(memory_space=pltpu.HBM)
    vmem = pl.BlockSpec(memory_space=pltpu.VMEM)
    return pl.pallas_call(
        functools.partial(kernel, dims),
        out_shape=jax.ShapeDtypeStruct((rows, cols, width), bf16),
        in_specs=[any_space]*5,
        out_specs=vmem,
        scratch_shapes=[
            pltpu.VMEM((1, width), jnp.float32),
            pltpu.VMEM((1, width), jnp.float32),
            pltpu.VMEM((height, breadth), bf16),
            pltpu.VMEM((PATCH * group * rows * PATCH, lon_n * LANES), bf16),
            pltpu.VMEM((lat_n, lon_n, CELLS, (rows - 1) * LANES), bf16),
            pltpu.VMEM((lat_n, lon_n, CELLS, LANES), bf16),
            pltpu.VMEM((total, CELLS, (rows - 1) * LANES), bf16),
            pltpu.VMEM((total, CELLS, LANES), bf16),
            pltpu.VMEM((total, CELLS, LANES), bf16),
            pltpu.VMEM((total, PATCH, PATCH, width), bf16),
            pltpu.VMEM((total + 1, CELLS, width), bf16),
            pltpu.VMEM((3, 3, width, width), bf16),
            pltpu.VMEM((3, 3, tap_width if composed else CELLS, width), bf16),
            pltpu.VMEM((9, 8, width), jnp.float32),
            pltpu.VMEM(((rows + 2) * row_slots, 3 * tap_width), bf16),
            pltpu.SemaphoreType.DMA,
            pltpu.SemaphoreType.DMA,
            pltpu.SemaphoreType.DMA,
            pltpu.SemaphoreType.DMA,
            pltpu.SemaphoreType.DMA((9,)),
            pltpu.SemaphoreType.DMA,
            pltpu.SemaphoreType.DMA,
            pltpu.SemaphoreType.DMA,
            pltpu.SemaphoreType.DMA,
            pltpu.SemaphoreType.DMA,
            pltpu.SemaphoreType.DMA,
        ],
        compiler_params=pltpu.CompilerParams(
            collective_id=0, has_side_effects=True, vmem_limit_bytes=52 * 1024 * 1024
        ),
        name="tiles",
    )(
        *(pltpu.with_memory_space_constraint(v, pltpu.HBM) for v in (raw_fields, embed_weight, embed_bias.reshape(1, width), conv_weight, conv_bias.reshape(1, width))),
    )


def solution(mesh):
    return jax.shard_map(
        per_device,
        mesh=mesh,
        in_specs=(P(("lat", "lon"), None, None), P(), P(), P(), P()),
        out_specs=P("lat", "lon", None),
        check_vma=False,
    )
```

time: 36.8 us -> 33.3 us (0.905)
  Pallas kernels: 34.4 us -> 32.2 us
  local copies, waits for them, and re-layouts: 2.24 us -> 0.95 us
    pallas_call x1, Pallas kernels: 34.4 us -> 32.2 us  [per_device(): pl.pallas_call(functools.partial(kernel, dims), out_shape=jax.ShapeDtypeS...]
    unnamed x1, local copies, waits for them, and re-layouts: 2.24 us -> 0.95 us
where the time goes in v2:
time: 33.3 us; the launch traced here: 33.2 us
  Pallas kernels  32.2 us (97%)
  local copies, waits for them, and re-layouts  0.95 us (3%)
    pallas_call x1, Pallas kernels, per_device(): pl.pallas_call(functools.partial(kernel, dims), out_shape=jax.ShapeDtypeS...  32.2 us
    unnamed x1, local copies, waits for them, and re-layouts  0.95 us

profile of v2, /device:TPU:0, one launch (start us, length us, event | category | flops | bytes accessed | tf_op | source)
XLA Modules:
  0.0 33.2 jit_solution(12944651754431516278)
XLA Ops:
  0.0 32.2 %tiles.1 = bf16[5,90,1024]{2,1,0:T(8,128)(2,1)S(1)} custom-call(bf16[1,160,1440]{2,1,0:T(8,128)(2,1)} %raw_hbm.1, bf16[32,4,4,1024]{3,2,1,0:T(4,128)(2,1)} %ew_hbm.1, f32[1,1024]{1,0:T(1,128)} %bitcast.2, bf16[3,3,1024,1024]{3,2,1,0:T(8,128)(2,1)} %cw_hbm.1, f32[1,1024]{1,0:T(1,128)} %bitcast.3), custom_call_target="tpu_custom_call" | custom-call | tf_op jit(solution)/shard_map/tiles/pallas_call | solution.py:320
  32.2 0.9 %copy.7 = bf16[5,90,1024]{2,1,0:T(8,128)(2,1)} copy(bf16[5,90,1024]{2,1,0:T(8,128)(2,1)S(1)} %tiles.1) | data formatting | bytes 1843200

commit v3 on v2

--- a/solution.py
+++ b/solution.py
@@ -41,7 +41,7 @@
 
     barrier = pltpu.get_barrier_semaphore()
 
-    @pl.loop(0, total - 1)
+    @pl.loop(0, total - 1, unroll=total <= 32)
     def _(step):
         a, b = peer(step)
         pl.semaphore_signal(barrier, inc=1, device_id=(a, b), device_id_type=MESH)
@@ -166,7 +166,7 @@
     pl.semaphore_wait(barrier, total - 1)
 
     def exchange(source, dest, out_sem, in_sem):
-        @pl.loop(0, total - 1)
+        @pl.loop(0, total - 1, unroll=total <= 32)
         def _(step):
             a, b = peer(step)
             pltpu.make_async_remote_copy(
@@ -234,63 +234,62 @@
         for copy in cw_copies:
             copy.wait()
 
-    def row_bias(a, n):
+    def row_bias(a, n, scales):
         total_bias = cb_ref[:, pl.ds(n, step_n)]
         if composed:
             for p in range(3):
                 part = 0.0
                 for q in range(3):
                     part += bias[3 * p + q, 0:1, pl.ds(n, step_n)] + bias[3 * p + q, 1:2, pl.ds(n, step_n)]
-                if a + p == 0:
-                    part *= top
-                if a + p == rows + 1:
-                    part *= bottom
+                if scales is not None:
+                    part *= scales[p]
                 total_bias = total_bias + part
         return total_bias
 
-    def conv(first_rows):
+    def tap_rows(row, count):
+        if isinstance(row, int):
+            return taps[row * row_slots : (row + count) * row_slots, :]
+        return taps[pl.ds(pl.multiple_of(row * row_slots, 16), count * row_slots), :]
+
+    def conv(a, count, scales):
         @pl.loop(0, width // (2 * step_n))
         def _(block_n):
             for half in range(2):
                 n = pl.multiple_of(block_n * (2 * step_n) + half * step_n, step_n)
                 summed = None
                 for p in range(3):
-                    spans = [
-                        taps[(a + p) * row_slots : (a + p + count) * row_slots, :]
-                        for a, count in first_rows
-                    ]
-                    left = spans[0] if len(spans) == 1 else jnp.concatenate(spans, axis=0)
+                    left = tap_rows(a + p, count)
                     weights = kernel_weights[p, :, :, pl.ds(n, step_n)]
                     weights = weights.reshape(3 * tap_width, step_n)
                     part = jnp.dot(left, weights, preferred_element_type=jnp.float32)
                     summed = part if summed is None else summed + part
-                at = 0
-                for a, count in first_rows:
-                    shift = row_bias(a, n)
-                    for k in range(count):
-                        value = summed[at : at + row_slots] + shift
-                        value = 0.5 * value * (1.0 + lax.erf(value * (0.5 ** 0.5)))
-                        out_ref[a + k, :, pl.ds(n, step_n)] = value[:cols].astype(jnp.bfloat16)
-                        at += row_slots
-
-    conv([(1, rows - 2)])
-
-    pair_copy.wait_recv()
-    pltpu.make_async_copy(recv_far, recv_far, frecv_sem).wait()
+                shift = row_bias(a, n, scales)
+                for k in range(count):
+                    value = summed[k * row_slots : (k + 1) * row_slots] + shift
+                    value = 0.5 * value * (1.0 + lax.erf(value * (0.5 ** 0.5)))
+                    out_ref[a + k, :, pl.ds(n, step_n)] = value[:cols].astype(jnp.bfloat16)
+
+    conv(1, rows - 2, None)
+
     inside = top * bottom
-    for source, row, scale in (
-        (near, (rows + 1) * (1 - odd), None),
-        (recv_far, (rows + 1) * odd, inside),
-    ):
+    even = jnp.where(odd > 0, 0.0, 1.0)
+    scales = (1.0 - even * (1.0 - inside), 1.0, 1.0 - (1.0 - even) * (1.0 - inside))
+
+    def edge(source, below, factor, row_scales):
         x = source[...].reshape(total * CELLS, LANES).T[:row_slots]
         for n in range(0, tap_width, step_n):
             if composed:
                 e = x[:, n : n + step_n].astype(jnp.float32)
             else:
                 e = embed(x, n)
-                e = e if scale is None else e * scale
-            place(row, n, e)
-    conv([(0, 1), (rows - 1, 1)])
+                e = e if factor is None else e * factor
+            place((rows + 1) * below, n, e)
+        conv((rows - 1) * below, 1, row_scales)
+
+    pair_copy.wait_recv()
+    edge(near, 1 - odd, None, None)
+    pltpu.make_async_copy(recv_far, recv_far, frecv_sem).wait()
+    edge(recv_far, odd, inside, scales)
 
     sent = pl.ds(0, total - 1)
     pltpu.make_async_copy(recv.at[sent], recv.at[sent], send_sem).wait()

time: 33.3 us -> 32.7 us (0.982)
  Pallas kernels: 32.2 us -> 31.7 us
    pallas_call x1, Pallas kernels: 32.2 us -> 31.7 us  [per_device(): pl.pallas_call(functools.partial(kernel, dims), out_shape=jax.ShapeDtypeS...]
where the time goes in v3:
time: 32.7 us; the launch traced here: 32.6 us
  Pallas kernels  31.7 us (97%)
  local copies, waits for them, and re-layouts  0.95 us (3%)
    pallas_call x1, Pallas kernels, per_device(): pl.pallas_call(functools.partial(kernel, dims), out_shape=jax.ShapeDtypeS...  31.7 us
    unnamed x1, local copies, waits for them, and re-layouts  0.95 us

profile of v3, /device:TPU:0, one launch (start us, length us, event | category | flops | bytes accessed | tf_op | source)
XLA Modules:
  0.0 32.6 jit_solution(11777445558830234766)
XLA Ops:
  0.0 31.7 %tiles.1 = bf16[5,90,1024]{2,1,0:T(8,128)(2,1)S(1)} custom-call(bf16[1,160,1440]{2,1,0:T(8,128)(2,1)} %raw_hbm.1, bf16[32,4,4,1024]{3,2,1,0:T(4,128)(2,1)} %ew_hbm.1, f32[1,1024]{1,0:T(1,128)} %bitcast.2, bf16[3,3,1024,1024]{3,2,1,0:T(8,128)(2,1)} %cw_hbm.1, f32[1,1024]{1,0:T(1,128)} %bitcast.3), custom_call_target="tpu_custom_call" | custom-call | tf_op jit(solution)/shard_map/tiles/pallas_call | solution.py:319
  31.7 0.9 %copy.7 = bf16[5,90,1024]{2,1,0:T(8,128)(2,1)} copy(bf16[5,90,1024]{2,1,0:T(8,128)(2,1)S(1)} %tiles.1) | data formatting | bytes 1843200
